TPU v7x, 32 devices: a whole 2x2x4 slice. The times are simulated.
32 devices in a mesh: dp: 8 (over y, x, core), tensor: 4 (over z).
Axes of the slice: x: 2, y: 2, z: 4, core: 2. Of those that a mesh axis runs over, the one named last changes fastest.
Arguments:
- tokens: bfloat16 [6400, 1024], P('dp'), may hold values from -10.5 to 10.5, as said below
- blank_mask: int32 [64], P('dp'), may hold values 0 or 1
- norm_gain: float32 [2, 1024], replicated, may hold values from 0.25 to 1.75
- norm_bias: float32 [2, 1024], replicated, may hold values from -1.8 to 1.8
- w_qkv: bfloat16 [3, 1024, 1024], P(None, None, 'tensor'), may hold values from -0.1875 to 0.1875
- qv_bias: float32 [2, 1024], P(None, 'tensor'), may hold values from -1.8 to 1.8
- rel_bias: float32 [32, 361], P('tensor'), may hold values from -5 to 5
- w_out: bfloat16 [1024, 1024], P('tensor'), may hold values from -0.75 to 0.75
- out_bias: float32 [2, 1024], replicated, may hold values from -1.8 to 1.8
- w_up: bfloat16 [1024, 4096], P(None, 'tensor'), may hold values from -0.1875 to 0.1875
- up_bias: float32 [4096], P('tensor'), may hold values from -1.8 to 1.8
- w_down: bfloat16 [4096, 1024], P('tensor'), may hold values from -0.09375 to 0.09375
- grad_out: bfloat16 [6400, 1024], P('dp'), may hold values from -6 to 6
Outputs:
- output: bfloat16 [6400, 1024], P(('dp', 'tensor'))
- grad_tokens: float32 [6400, 1024], P(('dp', 'tensor'))
- grad_norm_gain: float32 [2, 1024], replicated
- grad_norm_bias: float32 [2, 1024], replicated
- grad_w_qkv: float32 [3, 1024, 1024], P(None, None, 'tensor')
- grad_qv_bias: float32 [2, 1024], P(None, 'tensor')
- grad_rel_bias: float32 [32, 361], P('tensor')
- grad_w_out: float32 [1024, 1024], P('tensor')
- grad_out_bias: float32 [2, 1024], replicated
- grad_w_up: float32 [1024, 4096], P(None, 'tensor')
- grad_up_bias: float32 [4096], P('tensor')
- grad_w_down: float32 [4096, 1024], P('tensor')
- root_means: float32 [3], replicated
Inputs may be any that keep to these rules, and one draw needn't show every extreme that they name: `tokens`: values are of order one, with row scales differing between windows. `blank_mask`: 1 marks a blank window.
All inputs are finite; a program needn't handle non-finite values. No bound on the sum of `blank_mask` on one device may be relied on, other than what follows from the above.
Results may differ from a plain program's by a relative error of at most 0.0095.
The roundings to bfloat16 on the way count: a program that leaves them out, or rounds other values in their place, can miss the bound.
Values may be sent and summed in bfloat16 or wider, within the bound.
A program may use at most 128 MiB of HBM per device.

v0:
```python
import jax
import jax.numpy as jnp
from jax import lax
from jax.sharding import PartitionSpec as P

WS = 10
highest = lax.Precision.HIGHEST
norm_eps = 1e-05
half_root = 0.7071067811865476
gauss_norm = 0.3989422804014327


def normalize(values):
    center = jnp.mean(values, axis=-1, keepdims=True)
    shifted = values - center
    spread = jnp.mean(shifted * shifted, axis=-1, keepdims=True)
    inverse = lax.rsqrt(spread + norm_eps)
    return (shifted * inverse, inverse)


def norm_back(gradient, normed_hat, inverse, gain_row):
    scaled = gradient * gain_row
    inner_sum = jnp.mean(scaled, axis=-1, keepdims=True)
    cross_sum = jnp.mean(scaled * normed_hat, axis=-1, keepdims=True)
    return inverse * (scaled - inner_sum - normed_hat * cross_sum)


def relative_onehot(window_side):
    positions = jnp.arange(window_side)
    offset_grid = positions[:, None] - positions[None, :] + (window_side - 1)
    return (offset_grid[:, :, None] == jnp.arange(2 * window_side - 1)[None, None, :]).astype(
        jnp.float32
    )


def relative(bias_table, window_side):
    onehot = relative_onehot(window_side)
    heads_count = bias_table.shape[0]
    square = bias_table.reshape(heads_count, 2 * window_side - 1, 2 * window_side - 1)
    spread_full = jnp.einsum("ija,klb,hab->hikjl", onehot, onehot, square, precision=highest)
    return spread_full.reshape(heads_count, window_side * window_side, window_side * window_side)


def relative_back(gradient, window_side):
    onehot = relative_onehot(window_side)
    heads_count = gradient.shape[0]
    grad_grid = gradient.reshape(heads_count, window_side, window_side, window_side, window_side)
    folded = jnp.einsum("hikjl,ija,klb->hab", grad_grid, onehot, onehot, precision=highest)
    return folded.reshape(heads_count, (2 * window_side - 1) ** 2)


def scatter_rows(part):
    sums = lax.psum_scatter(part.astype(jnp.bfloat16), "tensor", scatter_dimension=0, tiled=True)
    return sums.astype(jnp.float32)


def on_device(
    tokens,
    blank_mask,
    norm_gain,
    norm_bias,
    w_qkv,
    qv_bias,
    rel_bias,
    w_out,
    out_bias,
    w_up,
    up_bias,
    w_down,
    grad_out,
):
    tensor_count = lax.axis_size("tensor")
    rows_all = tokens.shape[0]
    rows_own = rows_all // tensor_count
    row_start = lax.axis_index("tensor") * rows_own
    window_area = WS * WS
    windows = rows_all // window_area
    heads_here = rel_bias.shape[0]
    width_here = w_out.shape[0]
    head_dim = width_here // heads_here
    score_scale = head_dim ** (-0.5)

    def own_rows(values):
        return lax.dynamic_slice_in_dim(values, row_start, rows_own, 0)

    source = tokens.astype(jnp.float32)
    hat_one, inv_one = normalize(source)
    normed_one = (hat_one * norm_gain[0] + norm_bias[0]).astype(jnp.bfloat16)
    projected = jnp.einsum("rd,tde->tre", normed_one, w_qkv, preferred_element_type=jnp.float32)
    shifts = jnp.stack([qv_bias[0], jnp.zeros_like(qv_bias[0]), qv_bias[1]])
    projected = (projected + shifts[:, None, :]).astype(jnp.bfloat16)
    projected = projected.reshape(3, windows, window_area, heads_here, head_dim)
    query_part, key_part, value_part = (projected[0], projected[1], projected[2])
    bias_block = relative(rel_bias, WS)

    def scores_of():
        raw_scores = jnp.einsum(
            "wihc,wjhc->whij", query_part, key_part, preferred_element_type=jnp.float32
        )
        return raw_scores * score_scale + bias_block[None]

    scores = scores_of()
    row_top = jnp.max(scores, axis=-1, keepdims=True)
    exponent = jnp.exp(scores - row_top)
    row_total = jnp.sum(exponent, axis=-1, keepdims=True)
    log_total = row_top + jnp.log(row_total)
    weights = (exponent / row_total).astype(jnp.bfloat16)
    mixed_heads = jnp.einsum(
        "whij,wjhc->wihc", weights, value_part, preferred_element_type=jnp.float32
    )
    mixed_heads = mixed_heads.astype(jnp.bfloat16).reshape(rows_all, width_here)
    attn_part = jnp.dot(mixed_heads, w_out, preferred_element_type=jnp.float32)
    alive_rows = jnp.repeat(1.0 - blank_mask.astype(jnp.float32), window_area)
    alive_own = own_rows(alive_rows)[:, None]
    source_own = own_rows(source)
    attn_own = scatter_rows(attn_part) + out_bias[0]
    resid_own = source_own + attn_own
    hat_two, inv_two = normalize(resid_own)
    normed_rows = (hat_two * norm_gain[1] + norm_bias[1]).astype(jnp.bfloat16)
    normed_two = lax.all_gather(normed_rows, "tensor", axis=0, tiled=True)
    hidden = jnp.dot(normed_two, w_up, preferred_element_type=jnp.float32) + up_bias
    active = jax.nn.gelu(hidden, approximate=False).astype(jnp.bfloat16)
    mlp_part = jnp.dot(active, w_down, preferred_element_type=jnp.float32)
    branch_own = scatter_rows(mlp_part) + out_bias[1]
    output = (resid_own + branch_own).astype(jnp.bfloat16)
    stat_terms = jnp.stack(
        [
            jnp.sum(alive_own * source_own * source_own),
            jnp.sum(alive_own * attn_own * attn_own),
            jnp.sum(alive_own * branch_own * branch_own),
            jnp.sum(alive_own),
        ]
    )
    stat_total = lax.psum(stat_terms, ("dp", "tensor"))
    grad_full = grad_out.astype(jnp.float32)
    grad_down = jnp.einsum("rf,rd->fd", active, grad_out, preferred_element_type=jnp.float32)
    grad_active = jnp.einsum("rd,fd->rf", grad_out, w_down, preferred_element_type=jnp.float32)
    gelu_slope = (
        0.5 * (1.0 + lax.erf(hidden * half_root))
        + hidden * jnp.exp(-0.5 * hidden * hidden) * gauss_norm
    )
    grad_hidden = (grad_active * gelu_slope).astype(jnp.bfloat16)
    grad_up_bias = jnp.sum(grad_hidden.astype(jnp.float32), axis=0)
    grad_up = jnp.einsum("rd,rf->df", normed_two, grad_hidden, preferred_element_type=jnp.float32)
    norm_part = jnp.einsum("rf,df->rd", grad_hidden, w_up, preferred_element_type=jnp.float32)
    grad_norm_own = scatter_rows(norm_part)
    grad_resid_own = own_rows(grad_full) + norm_back(grad_norm_own, hat_two, inv_two, norm_gain[1])
    grad_attn = lax.all_gather(grad_resid_own.astype(jnp.bfloat16), "tensor", axis=0, tiled=True)
    gain_two = jnp.sum(grad_norm_own * hat_two, axis=0)
    shift_two = jnp.sum(grad_norm_own, axis=0)
    attn_bias_term = jnp.sum(own_rows(grad_attn).astype(jnp.float32), axis=0)
    mlp_bias_term = jnp.sum(own_rows(grad_full), axis=0)
    grad_wout = jnp.einsum("re,rd->ed", mixed_heads, grad_attn, preferred_element_type=jnp.float32)
    grad_mixed = jnp.einsum("rd,ed->re", grad_attn, w_out, preferred_element_type=jnp.float32)
    grad_mixed = grad_mixed.astype(jnp.bfloat16).reshape(windows, window_area, heads_here, head_dim)
    probs_full = jnp.exp(scores_of() - log_total)
    probs_low = probs_full.astype(jnp.bfloat16)
    grad_values = jnp.einsum(
        "whij,wihc->wjhc", probs_low, grad_mixed, preferred_element_type=jnp.float32
    )
    grad_probs = jnp.einsum(
        "wihc,wjhc->whij", grad_mixed, value_part, preferred_element_type=jnp.float32
    )
    inner_sum = jnp.sum(grad_probs * probs_full, axis=-1, keepdims=True)
    grad_scores = (probs_full * (grad_probs - inner_sum)).astype(jnp.bfloat16)
    grad_table = relative_back(jnp.sum(grad_scores.astype(jnp.float32), axis=0), WS)
    grad_query = (
        jnp.einsum("whij,wjhc->wihc", grad_scores, key_part, preferred_element_type=jnp.float32)
        * score_scale
    )
    grad_keys = (
        jnp.einsum("whij,wihc->wjhc", grad_scores, query_part, preferred_element_type=jnp.float32)
        * score_scale
    )
    grad_proj = (
        jnp.stack([grad_query, grad_keys, grad_values])
        .astype(jnp.bfloat16)
        .reshape(3, rows_all, width_here)
    )
    grad_qv = jnp.stack(
        [
            jnp.sum(grad_proj[0].astype(jnp.float32), axis=0),
            jnp.sum(grad_proj[2].astype(jnp.float32), axis=0),
        ]
    )
    grad_qkv = jnp.einsum("rd,tre->tde", normed_one, grad_proj, preferred_element_type=jnp.float32)
    input_part = jnp.einsum("tre,tde->rd", grad_proj, w_qkv, preferred_element_type=jnp.float32)
    grad_in_own = scatter_rows(input_part)
    hat_one_own = own_rows(hat_one)
    grad_tokens = grad_resid_own + norm_back(
        grad_in_own, hat_one_own, own_rows(inv_one), norm_gain[0]
    )
    gain_one = jnp.sum(grad_in_own * hat_one_own, axis=0)
    shift_one = jnp.sum(grad_in_own, axis=0)
    gain_terms = jnp.stack([gain_one, gain_two])
    shift_terms = jnp.stack([shift_one, shift_two])
    bias_terms = jnp.stack([attn_bias_term, mlp_bias_term])
    gain_sums, shift_sums, bias_sums = lax.psum(
        (gain_terms, shift_terms, bias_terms), ("dp", "tensor")
    )
    grad_qv, grad_table, grad_up_bias = lax.psum((grad_qv, grad_table, grad_up_bias), "dp")
    grad_qkv, grad_wout, grad_up, grad_down = [
        total.astype(jnp.float32)
        for total in lax.psum(
            [part.astype(jnp.bfloat16) for part in (grad_qkv, grad_wout, grad_up, grad_down)], "dp"
        )
    ]
    live_count = jnp.maximum(stat_total[3], 1.0) * tokens.shape[1]
    root_means = jnp.sqrt(stat_total[0:3] / live_count)
    return (
        output,
        grad_tokens,
        gain_sums,
        shift_sums,
        grad_qkv,
        grad_qv,
        grad_table,
        grad_wout,
        bias_sums,
        grad_up,
        grad_up_bias,
        grad_down,
        root_means,
    )


def solution(mesh):
    in_specs = (
        P("dp", None),
        P("dp"),
        P(),
        P(),
        P(None, None, "tensor"),
        P(None, "tensor"),
        P("tensor", None),
        P("tensor", None),
        P(),
        P(None, "tensor"),
        P("tensor"),
        P("tensor", None),
        P("dp", None),
    )
    out_specs = (
        P(("dp", "tensor"), None),
        P(("dp", "tensor"), None),
        P(),
        P(),
        P(None, None, "tensor"),
        P(None, "tensor"),
        P("tensor", None),
        P("tensor", None),
        P(),
        P(None, "tensor"),
        P("tensor"),
        P("tensor", None),
        P(),
    )
    return jax.shard_map(
        on_device, mesh=mesh, in_specs=in_specs, out_specs=out_specs, check_vma=False
    )
```

profile of v0, /device:TPU:0, one launch (start us, length us, event | category | flops | bytes accessed | tf_op | source)
XLA Modules:
  0.0 476.1 jit_solution(3866228508899291969)
XLA Ops:
  8.7 4.8 %convolution_bitcast_fusion = f32[8,10,10,10,10]{4,3,2,1,0:T(8,128)} fusion(f32[8,19,10,10,1]{1,3,4,2,0:T(8,128)S(1)} %convolution_bitcast_fusion.2, s32[10,10]{1,0:T(8,128)S(1)} %subtract_add_fusion), kind=kOutput, calls=%fused_computation.39 | convolution fusion | flops 18241900 | bytes 381200 | tf_op jit(solution)/shard_map/ija,klb,hab->hikjl/dot_general | solution.py:40
  13.5 4.4 reshape.173
  20.1 1.7 convert_reduce_fusion.2
  21.9 2.0 multiply_reduce_fusion.1
  24.1 1.7 fusion.24
  27.6 2.2 copy.67
  29.7 1.7 squeeze.13
  32.4 2.4 squeeze.12
  34.8 2.2 fusion.89
  39.6 3.0 convolution_convert_fusion.2
  42.8 3.5 convert_element_type.123
  46.4 35.6 %reduce-scatter.5.cloned.1.call-done = bf16[200,1024]{1,0:T(8,128)(2,1)} async-done(((bf16[800,1024]{1,0:T(8,128)(2,1)}), bf16[200,1024]{1,0:T(8,128)(2,1)}) %reduce-scatter.5.cloned.1.call-update) | async-done | bytes 409616 | tf_op jit(solution)/shard_map/reduce_scatter | solution.py:53
  81.9 1.5 fusion.82
  84.7 37.1 %all-gather.3.cloned.1.call-done = bf16[800,1024]{1,0:T(8,128)(2,1)} async-done(((bf16[200,1024]{1,0:T(8,128)(2,1)}), bf16[800,1024]{1,0:T(8,128)(2,1)}) %all-gather.3.cloned.1.call-update) | async-done | bytes 1638416 | tf_op jit(solution)/shard_map/all_gather | solution.py:120
  121.8 10.8 %fusion.2 = (bf16[800,1024]{1,0:T(8,128)(2,1)}, f32[800,1024]{1,0:T(8,128)S(1)}) fusion(f32[1024]{0:T(1024)S(1)} %copy-done.50, bf16[800,1024]{1,0:T(8,128)(2,1)} %all-gather.3.cloned.1.call-done, bf16[1024,1024]{1,0:T(8,128)(2,1)S(1)} %copy-done), kind=kOutput, calls=%fused_computation.11 | convolution fusion | flops 1731788800 | bytes 8654848 | tf_op jit(solution)/shard_map/dot_general | solution.py:121
  132.7 3.7 convert_reduce_fusion.1
  137.5 3.1 convolution_convert_fusion.3
  140.7 5.3 %convolution_convert_fusion.4 = bf16[800,1024]{1,0:T(8,128)(2,1)} fusion(bf16[800,1024]{1,0:T(8,128)(2,1)} %get-tuple-element.100, bf16[1024,1024]{1,0:T(8,128)(2,1)} %param.24), kind=kOutput, calls=%fused_computation.47 | convolution fusion | flops 1678540800 | bytes 5373952 | tf_op jit(solution)/shard_map/dot_general | solution.py:123
  146.9 29.1 %reduce-scatter.9.cloned.1.call-done = bf16[200,1024]{1,0:T(8,128)(2,1)} async-done(((bf16[800,1024]{1,0:T(8,128)(2,1)}), bf16[200,1024]{1,0:T(8,128)(2,1)}) %reduce-scatter.9.cloned.1.call-update) | async-done | bytes 409616 | tf_op jit(solution)/shard_map/reduce_scatter | solution.py:53
  176.1 2.1 fusion.50
  178.1 35.5 %reduce-scatter.7.cloned.1.call-done = bf16[200,1024]{1,0:T(8,128)(2,1)} async-done(((bf16[800,1024]{1,0:T(8,128)(2,1)}), bf16[200,1024]{1,0:T(8,128)(2,1)}) %reduce-scatter.7.cloned.1.call-update) | async-done | bytes 409616 | tf_op jit(solution)/shard_map/reduce_scatter | solution.py:53
  213.6 3.8 fusion.81
  217.8 5.3 %convolution_convert_fusion = bf16[1024,1024]{1,0:T(8,128)(2,1)} fusion(bf16[800,1024]{1,0:T(8,128)(2,1)} %get-tuple-element.100, bf16[800,1024]{1,0:T(8,128)(2,1)S(1)} %copy-done.26), kind=kOutput, calls=%fused_computation.43 | convolution fusion | flops 1678770176 | bytes 5373952 | tf_op jit(solution)/shard_map/rf,rd->fd/dot_general | solution.py:136
  223.1 3.7 convolution_convert_fusion.1
  226.8 27.8 %all-gather.5.cloned.1.call-done = bf16[800,1024]{1,0:T(8,128)(2,1)} async-done(((bf16[200,1024]{1,0:T(8,128)(2,1)}), bf16[800,1024]{1,0:T(8,128)(2,1)}) %all-gather.5.cloned.1.call-update) | async-done | bytes 1638416 | tf_op jit(solution)/shard_map/all_gather | solution.py:148
  254.7 2.9 convolution_convert_fusion.7
  257.6 2.0 copy.76
  259.6 2.4 reshape.158
  262.0 2.8 convert_reduce_fusion.5
  266.0 2.0 convert_reduce_fusion
  269.0 1.3 convert_reduce_fusion.6
  275.1 4.4 fusion.23
  279.5 1.5 convolution_convert_fusion.6
  282.0 4.1 bitcast_convert_fusion
  286.2 2.1 subtract_multiply_fusion
  288.3 2.6 pad_maximum_fusion.8
  291.1 4.0 reshape.174
  295.1 12.4 %copy.101 = f32[8,10,10,10,10]{4,3,1,2,0:T(8,128)} copy(f32[8,10,10,10,10]{2,1,4,3,0:T(8,128)} %reshape.174) | data formatting | bytes 640000 | tf_op jit(solution)/shard_map/reshape | solution.py:47
  307.4 8.3 %convolution_bitcast_fusion.1 = f32[19,8,10,10]{0,3,2,1:T(8,128)S(1)} fusion(f32[8,10,10,10,10]{4,3,1,2,0:T(8,128)} %copy.101, s32[10,10]{1,0:T(8,128)S(1)} %copy-done.24), kind=kOutput, calls=%fused_computation.62 | convolution fusion | flops 18241900 | bytes 381200 | tf_op jit(solution)/shard_map/hikjl,ija,klb->hab/dot_general | solution.py:48
  316.5 25.3 %all-reduce.1 = (f32[2,256]{1,0:T(2,128)}, f32[8,361]{1,0:T(8,128)}, f32[1024]{0:T(1024)}) all-reduce(f32[2,256]{1,0:T(2,128)S(1)} %pad_maximum_fusion.7, f32[8,361]{1,0:T(8,128)S(1)} %reshape.160, f32[1024]{0:T(1024)S(1)} %copy-done.45), channel_id=1, replica_groups=mesh['dp'=8,'tensor'=4] {'dp'}, use_global_device_ids=true, to_apply=%region_24.0 | all-reduce | flops 4424 | bytes 35392 | tf_op jit(solution)/shard_map/psum | solution.py:201
  341.8 42.5 %all-reduce.5.cloned.1.call-done = (bf16[3,1024,256]{1,2,0:T(8,128)(2,1)}, bf16[256,1024]{1,0:T(8,128)(2,1)}, bf16[1024,1024]{1,0:T(8,128)(2,1)}, bf16[1024,1024]{1,0:T(8,128)(2,1)}) async-done(((bf16[3,1024,256]{1,2,0:T(8,128)(2,1)}, bf16[256,1024]{1,0:T(8,128)(2,1)}, bf16[1024,1024]{1,0:T(8,128)(2,1)}, bf16[1024,1024]{1,0:T(8,128)(2,1)}), (bf16[3,1024,256]{1,2,0:T(8,128)(2,1)}, ...) | async-done | bytes 6291472 | tf_op jit(solution)/shard_map/psum | solution.py:204
  384.4 3.2 copy.93
  388.7 2.5 convert_element_type.157
  391.2 2.5 convert_element_type.160
  393.7 29.6 %reduce-scatter.11.cloned.1.call-done = bf16[200,1024]{1,0:T(8,128)(2,1)} async-done(((bf16[800,1024]{1,0:T(8,128)(2,1)}), bf16[200,1024]{1,0:T(8,128)(2,1)}) %reduce-scatter.11.cloned.1.call-update) | async-done | bytes 409616 | tf_op jit(solution)/shard_map/reduce_scatter | solution.py:53
  423.3 1.7 fusion.51
  425.1 39.7 %all-reduce = (f32[2,1024]{1,0:T(2,128)}, f32[2,1024]{1,0:T(2,128)}, f32[2,1024]{1,0:T(2,128)}, f32[4]{0:T(128)S(1)}) all-reduce(f32[2,1024]{1,0:T(2,128)S(1)} %pad_maximum_fusion.3, f32[2,1024]{1,0:T(2,128)S(1)} %pad_maximum_fusion.4, f32[2,1024]{1,0:T(2,128)S(1)} %pad_maximum_fusion.5, ...), channel_id=1, replica_groups=mesh['dp'=8,'tensor'=4] {'dp','tensor'}, use_global_device_ids=true, to_apply=%region_17.0 | all-reduce | flops 6148 | bytes 49184 | tf_op jit(solution)/shard_map/psum | solution.py:198
  466.6 2.4 fusion.45
  (178 shorter events, 24.3 us)
Async XLA Ops:
  7.2 114.6 %copy-start = (bf16[1024,1024]{1,0:T(8,128)(2,1)S(1)}, bf16[1024,1024]{1,0:T(8,128)(2,1)}, u32[]{:S(2)}) copy-start(bf16[1024,1024]{1,0:T(8,128)(2,1)} %param.22) | copy-start | bytes 6291460
  7.2 74.7 %reduce-scatter.5.cloned.1.call-start = ((), (), s32[]{:S(2)}) async-start(), calls=%async_computation.4 | async-start | bytes 2048000 | tf_op jit(solution)/shard_map/reduce_scatter | solution.py:53
  13.5 5.4 %copy-start.46 = (f32[2,256]{1,0:T(2,128)S(1)}, f32[2,256]{1,0:T(2,128)}, u32[]{:S(2)}) copy-start(f32[2,256]{1,0:T(2,128)} %param.18) | copy-start | bytes 6148
  13.5 5.4 %copy-start.41 = (f32[2,1024]{1,0:T(2,128)S(1)}, f32[2,1024]{1,0:T(2,128)}, u32[]{:S(2)}) copy-start(f32[2,1024]{1,0:T(2,128)} %param.16) | copy-start | bytes 24580
  13.5 6.0 %copy-start.42 = (f32[2,1024]{1,0:T(2,128)S(1)}, f32[2,1024]{1,0:T(2,128)}, u32[]{:S(2)}) copy-start(f32[2,1024]{1,0:T(2,128)} %param.15) | copy-start | bytes 24580
  18.9 5.2 %copy-start.4 = (bf16[800,1024]{1,0:T(8,128)(2,1)S(1)}, bf16[800,1024]{1,0:T(8,128)(2,1)}, u32[]{:S(2)}) copy-start(bf16[800,1024]{1,0:T(8,128)(2,1)} %param.13) | copy-start | bytes 4915204
  18.9 5.2 %copy-start.49 = (bf16[3,1024,256]{2,1,0:T(8,128)(2,1)S(1)}, bf16[3,1024,256]{2,1,0:T(8,128)(2,1)}, u32[]{:S(2)}) copy-start(bf16[3,1024,256]{2,1,0:T(8,128)(2,1)} %param.17) | copy-start | bytes 4718596
  19.5 4.6 copy-start.44
  20.1 5.7 %copy-start.31 = (f32[1,1024]{1,0:T(1,128)}, f32[1,1024]{1,0:T(1,128)S(1)}, u32[]{:S(2)}) copy-start(f32[1,1024]{1,0:T(1,128)S(1)} %get-tuple-element.93) | copy-start | bytes 12292
  21.9 3.9 copy-start.29
  27.6 9.5 %copy-start.6 = (bf16[8,100,8,32]{1,0,3,2:T(8,128)(2,1)}, bf16[8,100,8,32]{1,0,3,2:T(8,128)(2,1)S(1)}, u32[]{:S(2)}) copy-start(bf16[8,100,8,32]{1,0,3,2:T(8,128)(2,1)S(1)} %squeeze.14) | copy-start | bytes 1228804
  31.4 5.6 %copy-start.8 = (bf16[8,100,8,32]{1,0,3,2:T(8,128)(2,1)}, bf16[8,100,8,32]{1,0,3,2:T(8,128)(2,1)S(1)}, u32[]{:S(2)}) copy-start(bf16[8,100,8,32]{1,0,3,2:T(8,128)(2,1)S(1)} %squeeze.13) | copy-start | bytes 1228804
  39.5 6.8 %copy-start.16 = (bf16[800,256]{0,1:T(8,128)(2,1)}, bf16[800,256]{0,1:T(8,128)(2,1)S(1)}, u32[]{:S(2)}) copy-start(bf16[800,256]{0,1:T(8,128)(2,1)S(1)} %reshape.157) | copy-start | bytes 1228804
  42.6 3.8 copy-start.43
  42.6 41.1 %copy-start.28 = (f32[1,1024]{1,0:T(1,128)S(1)}, f32[1,1024]{1,0:T(1,128)}, u32[]{:S(2)}) copy-start(f32[1,1024]{1,0:T(1,128)} %get-tuple-element.92) | copy-start | bytes 12292
  42.6 41.1 %copy-start.39 = (f32[1,1024]{1,0:T(1,128)S(1)}, f32[1,1024]{1,0:T(1,128)}, u32[]{:S(2)}) copy-start(f32[1,1024]{1,0:T(1,128)} %get-tuple-element.94) | copy-start | bytes 12292
  42.6 79.2 %all-gather.3.cloned.1.call-start = ((), (), s32[]{:S(2)}) async-start(), calls=%async_computation.5 | async-start | bytes 2048000 | tf_op jit(solution)/shard_map/all_gather | solution.py:120
  46.4 75.5 %copy-start.50 = (f32[1024]{0:T(1024)S(1)}, f32[1024]{0:T(1024)}, u32[]{:S(2)}) copy-start(f32[1024]{0:T(1024)} %param.23) | copy-start | bytes 12292
  84.7 91.4 %reduce-scatter.9.cloned.1.call-start = ((), (), s32[]{:S(2)}) async-start(), calls=%async_computation.7 | async-start | bytes 2048000 | tf_op jit(solution)/shard_map/reduce_scatter | solution.py:53
  121.8 10.8 %copy-start.25 = (bf16[800,1024]{1,0:T(8,128)(2,1)S(1)}, bf16[800,1024]{1,0:T(8,128)(2,1)}, u32[]{:S(2)}) copy-start(bf16[800,1024]{1,0:T(8,128)(2,1)} %param.25) | copy-start | bytes 4915204
  121.8 10.8 %copy-start.47 = (bf16[1024,1024]{1,0:T(8,128)(2,1)S(1)}, bf16[1024,1024]{1,0:T(8,128)(2,1)}, u32[]{:S(2)}) copy-start(bf16[1024,1024]{1,0:T(8,128)(2,1)} %param.24) | copy-start | bytes 6291460
  140.6 73.0 %reduce-scatter.7.cloned.1.call-start = ((), (), s32[]{:S(2)}) async-start(), calls=%async_computation.6 | async-start | bytes 2048000 | tf_op jit(solution)/shard_map/reduce_scatter | solution.py:53
  140.7 5.4 %copy-start.51 = (s32[8]{0:T(128)S(1)}, s32[8]{0:T(128)}, u32[]{:S(2)}) copy-start(s32[8]{0:T(128)} %param.14) | copy-start | bytes 100
  140.7 72.9 %copy-start.19 = (bf16[200,1024]{1,0:T(8,128)(2,1)S(1)}, bf16[200,1024]{1,0:T(8,128)(2,1)}, u32[]{:S(2)}) copy-start(bf16[200,1024]{1,0:T(8,128)(2,1)} %reduce-scatter.5.cloned.1.call-done) | copy-start | bytes 1228804
  140.7 72.9 %copy-start.26 = (bf16[800,1024]{1,0:T(8,128)(2,1)S(1)}, bf16[800,1024]{1,0:T(8,128)(2,1)}, u32[]{:S(2)}) copy-start(bf16[800,1024]{1,0:T(8,128)(2,1)} %param.25) | copy-start | bytes 4915204
  146.0 108.6 %all-gather.5.cloned.1.call-start = ((), (), s32[]{:S(2)}) async-start(), calls=%async_computation.8 | async-start | bytes 2048000 | tf_op jit(solution)/shard_map/all_gather | solution.py:148
  217.5 166.9 %all-reduce.5.cloned.1.call-start = ((), (), s32[]{:S(2)}) async-start(), calls=%async_computation.10 | async-start | bytes 12582912 | tf_op jit(solution)/shard_map/psum | solution.py:204
  217.8 5.3 %copy-start.48 = (bf16[800,1024]{1,0:T(8,128)(2,1)S(1)}, bf16[800,1024]{1,0:T(8,128)(2,1)}, u32[]{:S(2)}) copy-start(bf16[800,1024]{1,0:T(8,128)(2,1)} %all-gather.3.cloned.1.call-done) | copy-start | bytes 4915204
  217.8 5.3 %copy-start.53 = (bf16[800,1024]{1,0:T(8,128)(2,1)S(1)}, bf16[800,1024]{1,0:T(8,128)(2,1)}, u32[]{:S(2)}) copy-start(bf16[800,1024]{1,0:T(8,128)(2,1)} %copy-done.52) | copy-start | bytes 4915204
  226.8 35.2 %copy-start.3 = (f32[8,8,100,100]{2,3,1,0:T(8,128)S(1)}, f32[8,8,100,100]{2,3,1,0:T(8,128)}, u32[]{:S(2)}) copy-start(f32[8,8,100,100]{2,3,1,0:T(8,128)} %copy-done.2) | copy-start | bytes 7680004
  271.0 4.1 copy-start.5
  275.1 4.4 copy-start.17
  275.1 4.4 copy-start.27
  281.0 5.1 %copy-start.34 = (f32[800]{0:T(1024)S(1)}, f32[800]{0:T(1024)}, u32[]{:S(2)}) copy-start(f32[800]{0:T(1024)} %copy-done.33) | copy-start | bytes 9604
  281.1 5.2 %copy-start.30 = (f32[800]{0:T(1024)S(1)}, f32[800]{0:T(1024)}, u32[]{:S(2)}) copy-start(f32[800]{0:T(1024)} %copy-done.29) | copy-start | bytes 9604
  281.1 142.2 %reduce-scatter.11.cloned.1.call-start = ((), (), s32[]{:S(2)}) async-start(), calls=%async_computation.9 | async-start | bytes 2048000 | tf_op jit(solution)/shard_map/reduce_scatter | solution.py:53
  286.1 4.8 %copy-start.35 = (f32[8,32]{1,0:T(8,128)S(1)}, f32[8,32]{1,0:T(8,128)}, u32[]{:S(2)}) copy-start(f32[8,32]{1,0:T(8,128)} %get-tuple-element.104) | copy-start | bytes 3076
  286.1 4.9 %copy-start.36 = (f32[8,32]{1,0:T(8,128)S(1)}, f32[8,32]{1,0:T(8,128)}, u32[]{:S(2)}) copy-start(f32[8,32]{1,0:T(8,128)} %get-tuple-element.106) | copy-start | bytes 3076
  286.1 5.0 %copy-start.18 = (f32[8,100,100]{1,2,0:T(8,128)S(1)}, f32[8,100,100]{1,2,0:T(8,128)}, u32[]{:S(2)}) copy-start(f32[8,100,100]{1,2,0:T(8,128)} %get-tuple-element.74) | copy-start | bytes 960004
  295.1 12.4 %copy-start.24 = (s32[10,10]{1,0:T(8,128)S(1)}, s32[10,10]{1,0:T(8,128)}, u32[]{:S(2)}) copy-start(s32[10,10]{1,0:T(8,128)} %copy-done.23) | copy-start | bytes 1204
  307.4 9.1 %copy-start.45 = (f32[1024]{0:T(1024)S(1)}, f32[1024]{0:T(1024)}, u32[]{:S(2)}) copy-start(f32[1024]{0:T(1024)} %get-tuple-element.108) | copy-start | bytes 12292
  384.4 4.3 copy-start.13
  391.2 32.1 %copy-start.32 = (f32[1,1024]{1,0:T(1,128)S(1)}, f32[1,1024]{1,0:T(1,128)}, u32[]{:S(2)}) copy-start(f32[1,1024]{1,0:T(1,128)} %copy-done.31) | copy-start | bytes 12292
  391.2 33.9 %copy-start.38 = (f32[1024]{0:T(1024)S(1)}, f32[1024]{0:T(1024)}, u32[]{:S(2)}) copy-start(f32[1024]{0:T(1024)} %get-tuple-element.54) | copy-start | bytes 12292
  391.2 33.9 %copy-start.37 = (f32[1024]{0:T(1024)S(1)}, f32[1024]{0:T(1024)}, u32[]{:S(2)}) copy-start(f32[1024]{0:T(1024)} %get-tuple-element.59) | copy-start | bytes 12292
  391.2 33.9 %copy-start.40 = (f32[1024]{0:T(1024)S(1)}, f32[1024]{0:T(1024)}, u32[]{:S(2)}) copy-start(f32[1024]{0:T(1024)} %get-tuple-element.82) | copy-start | bytes 12292
  391.2 75.4 %copy-start.11 = (f32[200,1024]{1,0:T(8,128)S(1)}, f32[200,1024]{1,0:T(8,128)}, u32[]{:S(2)}) copy-start(f32[200,1024]{1,0:T(8,128)} %get-tuple-element.79) | copy-start | bytes 2457604
  391.2 77.8 %copy-start.1 = (bf16[1024,1024]{1,0:T(8,128)(2,1)S(1)}, bf16[1024,1024]{1,0:T(8,128)(2,1)}, u32[]{:S(2)}) copy-start(bf16[1024,1024]{1,0:T(8,128)(2,1)} %param.22) | copy-start | bytes 6291460
  (13 other events, 29.4 us)
Sparse Core Ops, SparseCore 0:
  42.7 39.1 reduce-scatter.4
  84.8 36.9 all-gather.2
  140.7 35.2 reduce-scatter.8
  178.2 35.3 reduce-scatter.6
  217.6 36.9 all-gather.4
  281.2 103.1 all-reduce.4
  386.7 36.5 reduce-scatter.10
where the time goes:
time: 485 us; the launch traced here: 476 us
  waiting for transfers between devices  237 us (49%)
  matrix products  73 us (15%)
  blocking collectives  65 us (13%)
  local copies, waits for them, and re-layouts  49.5 us (10%)
  other arithmetic  34.9 us (7%)
  between operations  15.6 us (3%)
    reduce_scatter x4, waiting for transfers between devices, scatter_rows(): lax.psum_scatter(part.astype(jnp.bfloat16), 'tensor', scatter_dimension=0...  130 us
    psum x1, waiting for transfers between devices, on_device(): lax.psum([part.astype(jnp.bfloat16) for part in (grad_qkv, grad_wout, gra...  42.5 us
    psum x1, blocking collectives, on_device(): lax.psum((gain_terms, shift_terms, bias_terms), ('dp', 'tensor'))  39.7 us
    all_gather x1, waiting for transfers between devices, on_device(): normed_two = lax.all_gather(normed_rows, 'tensor', axis=0, tiled=True)  37.1 us
    all_gather x1, waiting for transfers between devices, on_device(): lax.all_gather(grad_resid_own.astype(jnp.bfloat16), 'tensor', axis=0, til...  27.8 us
    psum x1, blocking collectives, on_device(): lax.psum((grad_qv, grad_table, grad_up_bias), 'dp')  25.3 us
    reshape x2, local copies, waits for them, and re-layouts, relative_back(): gradient.reshape(heads_count, window_side, window_side, window_side, wind...  16.3 us
    dot_general x1, matrix products, on_device(): jnp.dot(normed_two, w_up, preferred_element_type=jnp.float32) + up_bias  10.8 us
  transfers between devices with their start and end apart: 7, of which 7 were waited for; matrix products, arithmetic and copies ran while one was open for 14% of the time, Pallas kernels for 0%

commit v1 on v0

--- a/solution.py
+++ b/solution.py
@@ -8,6 +8,19 @@
 norm_eps = 1e-05
 half_root = 0.7071067811865476
 gauss_norm = 0.3989422804014327
+
+
+def gather_around(array, axis, dim):
+    devices, index, rows = (lax.axis_size(axis), lax.axis_index(axis), array.shape[dim])
+    upward = [(i, (i + 1) % devices) for i in range(devices)]
+    result = jnp.zeros((*array.shape[:dim], devices * rows, *array.shape[dim + 1 :]), array.dtype)
+    held = array
+    for step in range(devices):
+        owner = (index - step) % devices
+        result = lax.dynamic_update_slice_in_dim(result, held, owner * rows, axis=dim)
+        if step < devices - 1:
+            held = lax.ppermute(held, axis, upward)
+    return result
 
 
 def normalize(values):
@@ -145,7 +158,7 @@
     norm_part = jnp.einsum("rf,df->rd", grad_hidden, w_up, preferred_element_type=jnp.float32)
     grad_norm_own = scatter_rows(norm_part)
     grad_resid_own = own_rows(grad_full) + norm_back(grad_norm_own, hat_two, inv_two, norm_gain[1])
-    grad_attn = lax.all_gather(grad_resid_own.astype(jnp.bfloat16), "tensor", axis=0, tiled=True)
+    grad_attn = gather_around(grad_resid_own.astype(jnp.bfloat16), "tensor", 0)
     gain_two = jnp.sum(grad_norm_own * hat_two, axis=0)
     shift_two = jnp.sum(grad_norm_own, axis=0)
     attn_bias_term = jnp.sum(own_rows(grad_attn).astype(jnp.float32), axis=0)

time: 485 us -> 488 us (level)
    all_gather x1 -> x0, waiting for transfers between devices: 27.8 us -> none  [on_device(): lax.all_gather(grad_resid_own.astype(jnp.bfloat16), 'tensor', axis=0, til...]
    ppermute x0 -> x3, waiting for transfers between devices: none -> 24.5 us  [gather_around(): held = lax.ppermute(held, axis, upward)]
  transfers between devices with their start and end apart: 7 -> 9, of which waited for: 7 -> 9; matrix products, arithmetic and copies ran while one was open for 14% -> 14% of each run, Pallas kernels for 0% -> 0%
where the time goes in v1:
time: 488 us; the launch traced here: 479 us
  waiting for transfers between devices  236 us (48%)
  matrix products  74.1 us (15%)
  blocking collectives  63.6 us (13%)
  local copies, waits for them, and re-layouts  52.8 us (11%)
  other arithmetic  35.9 us (7%)
  between operations  15.6 us (3%)
    reduce_scatter x4, waiting for transfers between devices, scatter_rows(): lax.psum_scatter(part.astype(jnp.bfloat16), 'tensor', scatter_dimension=0...  132 us
    psum x1, waiting for transfers between devices, on_device(): lax.psum([part.astype(jnp.bfloat16) for part in (grad_qkv, grad_wout, gra...  42.1 us
    psum x1, blocking collectives, on_device(): lax.psum((gain_terms, shift_terms, bias_terms), ('dp', 'tensor'))  39.8 us
    all_gather x1, waiting for transfers between devices, on_device(): normed_two = lax.all_gather(normed_rows, 'tensor', axis=0, tiled=True)  37.1 us
    ppermute x3, waiting for transfers between devices, gather_around(): held = lax.ppermute(held, axis, upward)  24.5 us
    psum x1, blocking collectives, on_device(): lax.psum((grad_qv, grad_table, grad_up_bias), 'dp')  23.9 us
    reshape x2, local copies, waits for them, and re-layouts, relative_back(): gradient.reshape(heads_count, window_side, window_side, window_side, wind...  16.3 us
    dot_general x1, matrix products, on_device(): jnp.dot(normed_two, w_up, preferred_element_type=jnp.float32) + up_bias  10.8 us
  transfers between devices with their start and end apart: 9, of which 9 were waited for; matrix products, arithmetic and copies ran while one was open for 14% of the time, Pallas kernels for 0%

profile of v1, /device:TPU:0, one launch (start us, length us, event | category | flops | bytes accessed | tf_op | source)
XLA Modules:
  0.0 478.7 jit_solution(6745564054370685773)
XLA Ops:
  8.7 4.8 %convolution_bitcast_fusion = f32[8,10,10,10,10]{4,3,2,1,0:T(8,128)} fusion(f32[8,19,10,10,1]{1,3,4,2,0:T(8,128)S(1)} %convolution_bitcast_fusion.2, s32[10,10]{1,0:T(8,128)S(1)} %subtract_add_fusion), kind=kOutput, calls=%fused_computation.39 | convolution fusion | flops 18241900 | bytes 381200 | tf_op jit(solution)/shard_map/ija,klb,hab->hikjl/dot_general | solution.py:53
  13.5 4.4 reshape.173
  20.1 1.7 convert_reduce_fusion.2
  21.9 2.0 multiply_reduce_fusion.1
  24.1 1.7 fusion.24
  27.6 2.2 copy.67
  29.7 1.7 squeeze.13
  32.4 2.4 squeeze.12
  34.8 2.2 fusion.88
  39.6 3.0 convolution_convert_fusion.2
  42.8 3.5 convert_element_type.123
  46.4 35.5 %reduce-scatter.5.cloned.1.call-done = bf16[200,1024]{1,0:T(8,128)(2,1)} async-done(((bf16[800,1024]{1,0:T(8,128)(2,1)}), bf16[200,1024]{1,0:T(8,128)(2,1)}) %reduce-scatter.5.cloned.1.call-update) | async-done | bytes 409616 | tf_op jit(solution)/shard_map/reduce_scatter | solution.py:66
  84.7 37.1 %all-gather.2.cloned.1.call-done = bf16[800,1024]{1,0:T(8,128)(2,1)} async-done(((bf16[200,1024]{1,0:T(8,128)(2,1)}), bf16[800,1024]{1,0:T(8,128)(2,1)}) %all-gather.2.cloned.1.call-update) | async-done | bytes 1638416 | tf_op jit(solution)/shard_map/all_gather | solution.py:133
  121.8 10.8 %fusion.2 = (bf16[800,1024]{1,0:T(8,128)(2,1)}, f32[800,1024]{1,0:T(8,128)S(1)}) fusion(f32[1024]{0:T(1024)S(1)} %copy-done.50, bf16[800,1024]{1,0:T(8,128)(2,1)} %all-gather.2.cloned.1.call-done, bf16[1024,1024]{1,0:T(8,128)(2,1)S(1)} %copy-done), kind=kOutput, calls=%fused_computation.11 | convolution fusion | flops 1731788800 | bytes 8654848 | tf_op jit(solution)/shard_map/dot_general | solution.py:134
  132.6 3.7 convert_reduce_fusion.1
  137.5 3.1 convolution_convert_fusion.3
  140.7 5.2 %convolution_convert_fusion.4 = bf16[800,1024]{1,0:T(8,128)(2,1)} fusion(bf16[800,1024]{1,0:T(8,128)(2,1)} %get-tuple-element.100, bf16[1024,1024]{1,0:T(8,128)(2,1)} %param.24), kind=kOutput, calls=%fused_computation.47 | convolution fusion | flops 1678540800 | bytes 5373952 | tf_op jit(solution)/shard_map/dot_general | solution.py:136
  146.8 29.2 %reduce-scatter.9.cloned.1.call-done = bf16[200,1024]{1,0:T(8,128)(2,1)} async-done(((bf16[800,1024]{1,0:T(8,128)(2,1)}), bf16[200,1024]{1,0:T(8,128)(2,1)}) %reduce-scatter.9.cloned.1.call-update) | async-done | bytes 409616 | tf_op jit(solution)/shard_map/reduce_scatter | solution.py:66
  176.1 37.5 %reduce-scatter.7.cloned.1.call-done = bf16[200,1024]{1,0:T(8,128)(2,1)} async-done(((bf16[800,1024]{1,0:T(8,128)(2,1)}), bf16[200,1024]{1,0:T(8,128)(2,1)}) %reduce-scatter.7.cloned.1.call-update) | async-done | bytes 409616 | tf_op jit(solution)/shard_map/reduce_scatter | solution.py:66
  213.6 3.3 fusion.50
  218.3 2.4 constant_dynamic-update-slice_fusion.3
  221.0 12.3 %collective-permute-done = bf16[200,1024]{1,0:T(8,128)(2,1)S(1)} collective-permute-done((bf16[200,1024]{1,0:T(8,128)(2,1)S(1)}, bf16[200,1024]{1,0:T(8,128)(2,1)S(1)}, u32[]{:S(2)}, u32[]{:S(2)}) %collective-permute-start) | collective-permute-done | bytes 409632 | tf_op jit(solution)/shard_map/ppermute | solution.py:22
  233.4 5.1 %convolution_convert_fusion = bf16[1024,1024]{1,0:T(8,128)(2,1)} fusion(bf16[800,1024]{1,0:T(8,128)(2,1)} %get-tuple-element.100, bf16[800,1024]{1,0:T(8,128)(2,1)S(1)} %copy-done.24), kind=kOutput, calls=%fused_computation.43 | convolution fusion | flops 1678770176 | bytes 5373952 | tf_op jit(solution)/shard_map/rf,rd->fd/dot_general | solution.py:149
  238.5 6.6 %collective-permute-done.1 = bf16[200,1024]{1,0:T(8,128)(2,1)S(1)} collective-permute-done((bf16[200,1024]{1,0:T(8,128)(2,1)S(1)}, bf16[200,1024]{1,0:T(8,128)(2,1)S(1)}, u32[]{:S(2)}, u32[]{:S(2)}) %collective-permute-start.1) | collective-permute-done | bytes 409632 | tf_op jit(solution)/shard_map/ppermute | solution.py:22
  245.5 3.7 convolution_convert_fusion.1
  250.9 5.5 %collective-permute-done.2 = bf16[200,1024]{1,0:T(8,128)(2,1)S(1)} collective-permute-done((bf16[200,1024]{1,0:T(8,128)(2,1)S(1)}, bf16[200,1024]{1,0:T(8,128)(2,1)S(1)}, u32[]{:S(2)}, u32[]{:S(2)}) %collective-permute-start.2) | collective-permute-done | bytes 409632 | tf_op jit(solution)/shard_map/ppermute | solution.py:22
  257.2 2.8 convolution_convert_fusion.7
  260.0 2.0 copy.76
  262.0 2.4 reshape.158
  264.4 2.8 convert_reduce_fusion.5
  268.4 2.0 convert_reduce_fusion
  272.7 3.0 convolution_convert_fusion.6
  280.1 4.4 fusion.23
  285.5 4.1 bitcast_convert_fusion
  290.8 2.1 subtract_multiply_fusion
  292.9 2.7 pad_maximum_fusion.8
  295.7 4.0 reshape.174
  299.7 12.3 %copy.101 = f32[8,10,10,10,10]{4,3,1,2,0:T(8,128)} copy(f32[8,10,10,10,10]{2,1,4,3,0:T(8,128)} %reshape.174) | data formatting | bytes 640000 | tf_op jit(solution)/shard_map/reshape | solution.py:60
  312.0 8.3 %convolution_bitcast_fusion.1 = f32[19,8,10,10]{0,3,2,1:T(8,128)S(1)} fusion(f32[8,10,10,10,10]{4,3,1,2,0:T(8,128)} %copy.101, s32[10,10]{1,0:T(8,128)S(1)} %copy-done.28), kind=kOutput, calls=%fused_computation.62 | convolution fusion | flops 18241900 | bytes 381200 | tf_op jit(solution)/shard_map/hikjl,ija,klb->hab/dot_general | solution.py:61
  321.1 23.9 %all-reduce.1 = (f32[2,256]{1,0:T(2,128)}, f32[8,361]{1,0:T(8,128)}, f32[1024]{0:T(1024)}) all-reduce(f32[2,256]{1,0:T(2,128)S(1)} %pad_maximum_fusion.7, f32[8,361]{1,0:T(8,128)S(1)} %reshape.160, f32[1024]{0:T(1024)S(1)} %copy-done.45), channel_id=1, replica_groups=mesh['dp'=8,'tensor'=4] {'dp'}, use_global_device_ids=true, to_apply=%region_24.25 | all-reduce | flops 4424 | bytes 35392 | tf_op jit(solution)/shard_map/psum | solution.py:214
  345.0 42.1 %all-reduce.5.cloned.1.call-done = (bf16[3,1024,256]{1,2,0:T(8,128)(2,1)}, bf16[256,1024]{1,0:T(8,128)(2,1)}, bf16[1024,1024]{1,0:T(8,128)(2,1)}, bf16[1024,1024]{1,0:T(8,128)(2,1)}) async-done(((bf16[3,1024,256]{1,2,0:T(8,128)(2,1)}, bf16[256,1024]{1,0:T(8,128)(2,1)}, bf16[1024,1024]{1,0:T(8,128)(2,1)}, bf16[1024,1024]{1,0:T(8,128)(2,1)}), (bf16[3,1024,256]{1,2,0:T(8,128)(2,1)}, ...) | async-done | bytes 6291472 | tf_op jit(solution)/shard_map/psum | solution.py:217
  387.1 3.2 copy.93
  391.5 2.5 convert_element_type.157
  394.0 2.5 convert_element_type.160
  396.5 29.4 %reduce-scatter.11.cloned.1.call-done = bf16[200,1024]{1,0:T(8,128)(2,1)} async-done(((bf16[800,1024]{1,0:T(8,128)(2,1)}), bf16[200,1024]{1,0:T(8,128)(2,1)}) %reduce-scatter.11.cloned.1.call-update) | async-done | bytes 409616 | tf_op jit(solution)/shard_map/reduce_scatter | solution.py:66
  425.9 1.7 fusion.51
  427.7 39.8 %all-reduce = (f32[2,1024]{1,0:T(2,128)}, f32[2,1024]{1,0:T(2,128)}, f32[2,1024]{1,0:T(2,128)}, f32[4]{0:T(128)S(1)}) all-reduce(f32[2,1024]{1,0:T(2,128)S(1)} %pad_maximum_fusion.3, f32[2,1024]{1,0:T(2,128)S(1)} %pad_maximum_fusion.4, f32[2,1024]{1,0:T(2,128)S(1)} %pad_maximum_fusion.5, ...), channel_id=1, replica_groups=mesh['dp'=8,'tensor'=4] {'dp','tensor'}, use_global_device_ids=true, to_apply=%region_17.18 | all-reduce | flops 6148 | bytes 49184 | tf_op jit(solution)/shard_map/psum | solution.py:211
  469.2 2.4 fusion.45
  (186 shorter events, 31.9 us)
Async XLA Ops:
  7.2 114.6 %copy-start = (bf16[1024,1024]{1,0:T(8,128)(2,1)S(1)}, bf16[1024,1024]{1,0:T(8,128)(2,1)}, u32[]{:S(2)}) copy-start(bf16[1024,1024]{1,0:T(8,128)(2,1)} %param.22) | copy-start | bytes 6291460
  7.2 74.7 %reduce-scatter.5.cloned.1.call-start = ((), (), s32[]{:S(2)}) async-start(), calls=%async_computation.4 | async-start | bytes 2048000 | tf_op jit(solution)/shard_map/reduce_scatter | solution.py:66
  13.5 5.4 %copy-start.46 = (f32[2,256]{1,0:T(2,128)S(1)}, f32[2,256]{1,0:T(2,128)}, u32[]{:S(2)}) copy-start(f32[2,256]{1,0:T(2,128)} %param.18) | copy-start | bytes 6148
  13.5 5.4 %copy-start.41 = (f32[2,1024]{1,0:T(2,128)S(1)}, f32[2,1024]{1,0:T(2,128)}, u32[]{:S(2)}) copy-start(f32[2,1024]{1,0:T(2,128)} %param.16) | copy-start | bytes 24580
  13.5 6.0 %copy-start.42 = (f32[2,1024]{1,0:T(2,128)S(1)}, f32[2,1024]{1,0:T(2,128)}, u32[]{:S(2)}) copy-start(f32[2,1024]{1,0:T(2,128)} %param.15) | copy-start | bytes 24580
  18.9 5.2 %copy-start.4 = (bf16[800,1024]{1,0:T(8,128)(2,1)S(1)}, bf16[800,1024]{1,0:T(8,128)(2,1)}, u32[]{:S(2)}) copy-start(bf16[800,1024]{1,0:T(8,128)(2,1)} %param.13) | copy-start | bytes 4915204
  18.9 5.2 %copy-start.49 = (bf16[3,1024,256]{2,1,0:T(8,128)(2,1)S(1)}, bf16[3,1024,256]{2,1,0:T(8,128)(2,1)}, u32[]{:S(2)}) copy-start(bf16[3,1024,256]{2,1,0:T(8,128)(2,1)} %param.17) | copy-start | bytes 4718596
  19.5 4.6 copy-start.44
  20.1 5.7 %copy-start.32 = (f32[1,1024]{1,0:T(1,128)}, f32[1,1024]{1,0:T(1,128)S(1)}, u32[]{:S(2)}) copy-start(f32[1,1024]{1,0:T(1,128)S(1)} %get-tuple-element.93) | copy-start | bytes 12292
  21.9 3.9 copy-start.30
  27.6 9.5 %copy-start.6 = (bf16[8,100,8,32]{1,0,3,2:T(8,128)(2,1)}, bf16[8,100,8,32]{1,0,3,2:T(8,128)(2,1)S(1)}, u32[]{:S(2)}) copy-start(bf16[8,100,8,32]{1,0,3,2:T(8,128)(2,1)S(1)} %squeeze.14) | copy-start | bytes 1228804
  31.4 5.6 %copy-start.8 = (bf16[8,100,8,32]{1,0,3,2:T(8,128)(2,1)}, bf16[8,100,8,32]{1,0,3,2:T(8,128)(2,1)S(1)}, u32[]{:S(2)}) copy-start(bf16[8,100,8,32]{1,0,3,2:T(8,128)(2,1)S(1)} %squeeze.13) | copy-start | bytes 1228804
  39.5 6.8 %copy-start.16 = (bf16[800,256]{0,1:T(8,128)(2,1)}, bf16[800,256]{0,1:T(8,128)(2,1)S(1)}, u32[]{:S(2)}) copy-start(bf16[800,256]{0,1:T(8,128)(2,1)S(1)} %reshape.157) | copy-start | bytes 1228804
  42.6 3.8 copy-start.43
  42.6 41.1 %copy-start.29 = (f32[1,1024]{1,0:T(1,128)S(1)}, f32[1,1024]{1,0:T(1,128)}, u32[]{:S(2)}) copy-start(f32[1,1024]{1,0:T(1,128)} %get-tuple-element.92) | copy-start | bytes 12292
  42.6 41.1 %copy-start.40 = (f32[1,1024]{1,0:T(1,128)S(1)}, f32[1,1024]{1,0:T(1,128)}, u32[]{:S(2)}) copy-start(f32[1,1024]{1,0:T(1,128)} %get-tuple-element.94) | copy-start | bytes 12292
  42.6 79.2 %all-gather.2.cloned.1.call-start = ((), (), s32[]{:S(2)}) async-start(), calls=%async_computation.5 | async-start | bytes 2048000 | tf_op jit(solution)/shard_map/all_gather | solution.py:133
  46.4 75.4 %copy-start.50 = (f32[1024]{0:T(1024)S(1)}, f32[1024]{0:T(1024)}, u32[]{:S(2)}) copy-start(f32[1024]{0:T(1024)} %param.23) | copy-start | bytes 12292
  84.7 91.4 %reduce-scatter.9.cloned.1.call-start = ((), (), s32[]{:S(2)}) async-start(), calls=%async_computation.7 | async-start | bytes 2048000 | tf_op jit(solution)/shard_map/reduce_scatter | solution.py:66
  121.8 10.8 %copy-start.23 = (bf16[800,1024]{1,0:T(8,128)(2,1)S(1)}, bf16[800,1024]{1,0:T(8,128)(2,1)}, u32[]{:S(2)}) copy-start(bf16[800,1024]{1,0:T(8,128)(2,1)} %param.25) | copy-start | bytes 4915204
  121.8 10.8 %copy-start.47 = (bf16[1024,1024]{1,0:T(8,128)(2,1)S(1)}, bf16[1024,1024]{1,0:T(8,128)(2,1)}, u32[]{:S(2)}) copy-start(bf16[1024,1024]{1,0:T(8,128)(2,1)} %param.24) | copy-start | bytes 6291460
  140.6 73.0 %reduce-scatter.7.cloned.1.call-start = ((), (), s32[]{:S(2)}) async-start(), calls=%async_computation.6 | async-start | bytes 2048000 | tf_op jit(solution)/shard_map/reduce_scatter | solution.py:66
  140.7 5.3 %copy-start.51 = (s32[8]{0:T(128)S(1)}, s32[8]{0:T(128)}, u32[]{:S(2)}) copy-start(s32[8]{0:T(128)} %param.14) | copy-start | bytes 100
  140.7 72.9 %copy-start.20 = (bf16[200,1024]{1,0:T(8,128)(2,1)S(1)}, bf16[200,1024]{1,0:T(8,128)(2,1)}, u32[]{:S(2)}) copy-start(bf16[200,1024]{1,0:T(8,128)(2,1)} %reduce-scatter.5.cloned.1.call-done) | copy-start | bytes 1228804
  145.9 241.2 %all-reduce.5.cloned.1.call-start = ((), (), s32[]{:S(2)}) async-start(), calls=%async_computation.9 | async-start | bytes 12582912 | tf_op jit(solution)/shard_map/psum | solution.py:217
  176.1 42.3 %copy-start.19 = (bf16[200,1024]{1,0:T(8,128)(2,1)S(1)}, bf16[200,1024]{1,0:T(8,128)(2,1)}, u32[]{:S(2)}) copy-start(bf16[200,1024]{1,0:T(8,128)(2,1)} %reduce-scatter.9.cloned.1.call-done) | copy-start | bytes 1228804
  216.9 16.5 %copy-start.24 = (bf16[800,1024]{1,0:T(8,128)(2,1)S(1)}, bf16[800,1024]{1,0:T(8,128)(2,1)}, u32[]{:S(2)}) copy-start(bf16[800,1024]{1,0:T(8,128)(2,1)} %param.25) | copy-start | bytes 4915204
  220.8 12.6 %collective-permute-start = (bf16[200,1024]{1,0:T(8,128)(2,1)S(1)}, bf16[200,1024]{1,0:T(8,128)(2,1)S(1)}, u32[]{:S(2)}, u32[]{:S(2)}) collective-permute-start(bf16[200,1024]{1,0:T(8,128)(2,1)S(1)} %get-tuple-element.79), channel_id=1, source_target_pairs={{0,1},{1,2},{2,3},{3,0},{4,5},{5,6},{6,7},{7,4},{8,9},{9,10},{10,1... | collective-permute-start | bytes 1228808 | tf_op jit(solution)/shard_map/ppermute | solution.py:22
  221.0 24.5 %copy-start.48 = (bf16[800,1024]{1,0:T(8,128)(2,1)S(1)}, bf16[800,1024]{1,0:T(8,128)(2,1)}, u32[]{:S(2)}) copy-start(bf16[800,1024]{1,0:T(8,128)(2,1)} %all-gather.2.cloned.1.call-done) | copy-start | bytes 4915204
  221.0 24.5 %copy-start.53 = (bf16[800,1024]{1,0:T(8,128)(2,1)S(1)}, bf16[800,1024]{1,0:T(8,128)(2,1)}, u32[]{:S(2)}) copy-start(bf16[800,1024]{1,0:T(8,128)(2,1)} %copy-done.52) | copy-start | bytes 4915204
  233.4 11.7 %collective-permute-start.1 = (bf16[200,1024]{1,0:T(8,128)(2,1)S(1)}, bf16[200,1024]{1,0:T(8,128)(2,1)S(1)}, u32[]{:S(2)}, u32[]{:S(2)}) collective-permute-start(bf16[200,1024]{1,0:T(8,128)(2,1)S(1)} %collective-permute-done), channel_id=1, source_target_pairs={{0,1},{1,2},{2,3},{3,0},{4,5},{5,6},{6,7},{7,4},{8,9},{9,10},{10,1... | collective-permute-start | bytes 1228808 | tf_op jit(solution)/shard_map/ppermute | solution.py:22
  238.5 18.7 %copy-start.21 = (bf16[256,1024]{1,0:T(8,128)(2,1)S(1)}, bf16[256,1024]{1,0:T(8,128)(2,1)}, u32[]{:S(2)}) copy-start(bf16[256,1024]{1,0:T(8,128)(2,1)} %param.20) | copy-start | bytes 1572868
  245.1 11.3 %collective-permute-start.2 = (bf16[200,1024]{1,0:T(8,128)(2,1)S(1)}, bf16[200,1024]{1,0:T(8,128)(2,1)S(1)}, u32[]{:S(2)}, u32[]{:S(2)}) collective-permute-start(bf16[200,1024]{1,0:T(8,128)(2,1)S(1)} %collective-permute-done.1), channel_id=1, source_target_pairs={{0,1},{1,2},{2,3},{3,0},{4,5},{5,6},{6,7},{7,4},{8,9},{9,10},{10,1... | collective-permute-start | bytes 1228808 | tf_op jit(solution)/shard_map/ppermute | solution.py:22
  250.1 14.4 %copy-start.3 = (f32[8,8,100,100]{2,3,1,0:T(8,128)S(1)}, f32[8,8,100,100]{2,3,1,0:T(8,128)}, u32[]{:S(2)}) copy-start(f32[8,8,100,100]{2,3,1,0:T(8,128)} %copy-done.2) | copy-start | bytes 7680004
  284.5 5.1 %copy-start.35 = (f32[800]{0:T(1024)S(1)}, f32[800]{0:T(1024)}, u32[]{:S(2)}) copy-start(f32[800]{0:T(1024)} %copy-done.34) | copy-start | bytes 9604
  284.5 6.3 %copy-start.31 = (f32[800]{0:T(1024)S(1)}, f32[800]{0:T(1024)}, u32[]{:S(2)}) copy-start(f32[800]{0:T(1024)} %copy-done.30) | copy-start | bytes 9604
  284.6 141.3 %reduce-scatter.11.cloned.1.call-start = ((), (), s32[]{:S(2)}) async-start(), calls=%async_computation.8 | async-start | bytes 2048000 | tf_op jit(solution)/shard_map/reduce_scatter | solution.py:66
  289.6 6.0 %copy-start.36 = (f32[8,32]{1,0:T(8,128)S(1)}, f32[8,32]{1,0:T(8,128)}, u32[]{:S(2)}) copy-start(f32[8,32]{1,0:T(8,128)} %get-tuple-element.104) | copy-start | bytes 3076
  289.6 6.1 %copy-start.37 = (f32[8,32]{1,0:T(8,128)S(1)}, f32[8,32]{1,0:T(8,128)}, u32[]{:S(2)}) copy-start(f32[8,32]{1,0:T(8,128)} %get-tuple-element.106) | copy-start | bytes 3076
  289.6 6.2 %copy-start.18 = (f32[8,100,100]{1,2,0:T(8,128)S(1)}, f32[8,100,100]{1,2,0:T(8,128)}, u32[]{:S(2)}) copy-start(f32[8,100,100]{1,2,0:T(8,128)} %get-tuple-element.74) | copy-start | bytes 960004
  299.7 12.3 %copy-start.28 = (s32[10,10]{1,0:T(8,128)S(1)}, s32[10,10]{1,0:T(8,128)}, u32[]{:S(2)}) copy-start(s32[10,10]{1,0:T(8,128)} %copy-done.27) | copy-start | bytes 1204
  312.0 9.1 %copy-start.45 = (f32[1024]{0:T(1024)S(1)}, f32[1024]{0:T(1024)}, u32[]{:S(2)}) copy-start(f32[1024]{0:T(1024)} %get-tuple-element.108) | copy-start | bytes 12292
  387.1 4.3 copy-start.13
  393.9 31.9 %copy-start.33 = (f32[1,1024]{1,0:T(1,128)S(1)}, f32[1,1024]{1,0:T(1,128)}, u32[]{:S(2)}) copy-start(f32[1,1024]{1,0:T(1,128)} %copy-done.32) | copy-start | bytes 12292
  393.9 33.7 %copy-start.39 = (f32[1024]{0:T(1024)S(1)}, f32[1024]{0:T(1024)}, u32[]{:S(2)}) copy-start(f32[1024]{0:T(1024)} %get-tuple-element.54) | copy-start | bytes 12292
  393.9 33.7 %copy-start.38 = (f32[1024]{0:T(1024)S(1)}, f32[1024]{0:T(1024)}, u32[]{:S(2)}) copy-start(f32[1024]{0:T(1024)} %get-tuple-element.59) | copy-start | bytes 12292
  393.9 75.3 %copy-start.11 = (f32[200,1024]{1,0:T(8,128)S(1)}, f32[200,1024]{1,0:T(8,128)}, u32[]{:S(2)}) copy-start(f32[200,1024]{1,0:T(8,128)} %get-tuple-element.80) | copy-start | bytes 2457604
  394.0 77.7 %copy-start.1 = (bf16[1024,1024]{1,0:T(8,128)(2,1)S(1)}, bf16[1024,1024]{1,0:T(8,128)(2,1)}, u32[]{:S(2)}) copy-start(bf16[1024,1024]{1,0:T(8,128)(2,1)} %param.22) | copy-start | bytes 6291460
  (15 other events, 34.9 us)
Sparse Core Ops, SparseCore 0:
  42.7 39.1 reduce-scatter.4
  84.8 36.9 all-gather.1
  140.7 35.2 reduce-scatter.8
  178.2 35.3 reduce-scatter.6
  284.7 102.4 all-reduce.4
  389.3 36.5 reduce-scatter.10
